TPU v7x, 32 devices: a whole 2x2x4 slice. The times are simulated.
32 devices in a mesh: expert: 4 (over z), shard: 8 (over y, x, core).
Axes of the slice: x: 2, y: 2, z: 4, core: 2. Of those that a mesh axis runs over, the one named last changes fastest.
Arguments:
- master_gate: float32 [64, 2048, 1408], P('expert', 'shard'), may hold values from -0.1875 to 0.1875
- master_up: float32 [64, 2048, 1408], P('expert', 'shard'), may hold values from -0.1875 to 0.1875
- router_weight: float32 [2048, 64], P('shard', 'expert'), may hold values from -0.125 to 0.125
- router_gain: float32 [2048], P('shard'), may hold values from 0.25 to 1.75
Outputs:
- final_gate: bfloat16 [64, 2048, 1408], P('expert', None, 'shard')
- final_up: bfloat16 [64, 2048, 1408], P('expert', None, 'shard')
- scale_gate: float32 [64, 1408], P('expert', 'shard')
- scale_up: float32 [64, 1408], P('expert', 'shard')
- serve_router: bfloat16 [2048, 64], replicated
All inputs are finite; a program needn't handle non-finite values.
Results may differ from a plain program's by a relative error of at most 0.001.
Values may be sent and summed in bfloat16 or wider, within the bound.
A program may use at most 192 MiB of HBM per device.

v0:
```python
import jax
import jax.numpy as jnp
from jax import lax
from jax.sharding import PartitionSpec as P


def local(master_gate, master_up, router_weight, router_gain):
    total_gate, total_up = lax.psum(
        (jnp.sum(master_gate * master_gate, axis=1), jnp.sum(master_up * master_up, axis=1)),
        "shard",
    )
    scale_gate = jnp.sqrt(total_gate)
    scale_up = jnp.sqrt(total_up)
    narrow_gate, narrow_up = (
        (master_gate / jnp.expand_dims(scale_gate, 1)).astype(jnp.bfloat16),
        (master_up / jnp.expand_dims(scale_up, 1)).astype(jnp.bfloat16),
    )
    final_gate, final_up = (
        lax.all_to_all(narrow_gate, "shard", split_axis=2, concat_axis=1, tiled=True),
        lax.all_to_all(narrow_up, "shard", split_axis=2, concat_axis=1, tiled=True),
    )
    scale_gate = lax.dynamic_slice_in_dim(
        scale_gate, lax.axis_index("shard") * final_gate.shape[2], final_gate.shape[2], axis=1
    )
    scale_up = lax.dynamic_slice_in_dim(
        scale_up, lax.axis_index("shard") * final_up.shape[2], final_up.shape[2], axis=1
    )
    part_router = (router_weight * router_gain[:, None]).astype(jnp.bfloat16)
    row_router = lax.all_gather(part_router, "shard", axis=0, tiled=True)
    serve_router = lax.all_gather(row_router, "expert", axis=1, tiled=True)
    return (final_gate, final_up, scale_gate, scale_up, serve_router)


def solution(mesh):
    in_specs = (
        P("expert", "shard", None),
        P("expert", "shard", None),
        P("shard", "expert"),
        P("shard"),
    )
    out_specs = (
        P("expert", None, "shard"),
        P("expert", None, "shard"),
        P("expert", "shard"),
        P("expert", "shard"),
        P(),
    )
    return jax.shard_map(local, mesh=mesh, in_specs=in_specs, out_specs=out_specs, check_vma=False)
```

profile of v0, /device:TPU:0, one launch (start us, length us, event | category | flops | bytes accessed | tf_op | source)
XLA Modules:
  0.0 445.2 jit_solution(13781813590717320649)
XLA Ops:
  7.2 0.0 all-reduce.3.cloned.1.call-start
  7.2 15.8 %multiply_reduce_fusion = (f32[16,1408]{1,0:T(8,128)}, f32[16,1408]{1,0:T(8,128)}) fusion(f32[16,256,1408]{2,1,0:T(8,128)} %param.5, f32[16,256,1408]{2,1,0:T(8,128)} %param.4), kind=kLoop, calls=%fused_computation.1 | loop fusion | flops 23023616 | bytes 46317568 | tf_op jit(solution)/shard_map/reduce_sum | solution.py:9
  23.0 0.0 all-reduce.3.cloned.1.call-update
  23.1 23.7 %copy.22 = f32[16,256,1408]{1,0,2:T(8,128)} copy(f32[16,256,1408]{2,1,0:T(8,128)} %param.5) | data formatting | bytes 46137344 | tf_op args[1]
  46.8 32.3 %all-reduce.3.cloned.1.call-done = (f32[16,1408]{1,0:T(8,128)}, f32[16,1408]{1,0:T(8,128)}) async-done(((f32[16,1408]{1,0:T(8,128)}, f32[16,1408]{1,0:T(8,128)}), (f32[16,1408]{1,0:T(8,128)}, f32[16,1408]{1,0:T(8,128)})) %all-reduce.3.cloned.1.call-update) | async-done | bytes 180240 | tf_op jit(solution)/shard_map/psum | solution.py:8
  79.0 0.9 sqrt.7
  80.0 0.3 copy.21
  80.2 14.2 %divide_convert_fusion = bf16[16,256,1408]{1,0,2:T(8,128)(2,1)} fusion(f32[16,256,1408]{1,0,2:T(8,128)} %copy.22, f32[16,1408]{0,1:T(8,128)S(1)} %copy.21), kind=kLoop, calls=%fused_computation | loop fusion | flops 11534336 | bytes 34693120 | tf_op jit(solution)/shard_map/convert_element_type | solution.py:16
  94.4 5.2 %all-to-all-start.1 = ((bf16[16,256,1408]{1,0,2:T(8,128)(2,1)}), bf16[16,256,1408]{1,0,2:T(8,128)(2,1)}, u32[]{:S(2)}, u32[]{:S(2)}) async-start(bf16[16,256,1408]{1,0,2:T(8,128)(2,1)} %divide_convert_fusion), calls=%async_computation.1 | async-start | bytes 23068672 | tf_op jit(solution)/shard_map/all_to_all | solution.py:20
  99.7 23.7 %copy.18 = f32[16,256,1408]{1,0,2:T(8,128)} copy(f32[16,256,1408]{2,1,0:T(8,128)} %param.4) | data formatting | bytes 46137344 | tf_op args[0]
  123.4 0.3 copy.17
  123.7 0.0 copy-start.1
  123.7 14.2 %divide_convert_fusion.1 = bf16[16,256,1408]{1,0,2:T(8,128)(2,1)} fusion(f32[16,256,1408]{1,0,2:T(8,128)} %copy.18, f32[16,1408]{0,1:T(8,128)S(1)} %copy.17), kind=kLoop, calls=%fused_computation.2 | loop fusion | flops 11534336 | bytes 34693120 | tf_op jit(solution)/shard_map/convert_element_type | solution.py:15
  138.0 89.5 %all-to-all-done.1 = bf16[16,256,1408]{1,0,2:T(8,128)(2,1)} async-done(((bf16[16,256,1408]{1,0,2:T(8,128)(2,1)}), bf16[16,256,1408]{1,0,2:T(8,128)(2,1)}, u32[]{:S(2)}, u32[]{:S(2)}) %all-to-all-start.1) | async-done | bytes 11534368 | tf_op jit(solution)/shard_map/all_to_all | solution.py:20
  227.4 5.3 %all-to-all-start = ((bf16[16,256,1408]{1,0,2:T(8,128)(2,1)}), bf16[16,256,1408]{1,0,2:T(8,128)(2,1)}, u32[]{:S(2)}, u32[]{:S(2)}) async-start(bf16[16,256,1408]{1,0,2:T(8,128)(2,1)} %divide_convert_fusion.1), calls=%async_computation | async-start | bytes 23068672 | tf_op jit(solution)/shard_map/all_to_all | solution.py:19
  232.7 130.9 %all_gather.6 = bf16[2048,16]{0,1:T(8,128)(2,1)S(1)} all-gather(bf16[256,16]{0,1:T(8,128)(2,1)S(1)} %multiply_convert_fusion), channel_id=1, replica_groups=mesh['expert'=4,'shard'=8] {'shard'}, dimensions={0}, use_global_device_ids=true | all-gather | bytes 73728 | tf_op jit(solution)/shard_map/all_gather | solution.py:29
  363.6 14.0 %all_gather.7 = bf16[2048,64]{0,1:T(8,128)(2,1)S(1)} all-gather(bf16[2048,16]{0,1:T(8,128)(2,1)S(1)} %all_gather.6), channel_id=1, replica_groups=mesh['expert'=4,'shard'=8] {'expert'}, dimensions={1}, use_global_device_ids=true | all-gather | bytes 327680 | tf_op jit(solution)/shard_map/all_gather | solution.py:30
  377.6 0.7 constant_dynamic-slice_fusion
  378.3 0.7 constant_dynamic-slice_fusion.1
  379.0 11.4 %copy.24 = bf16[16,8,256,176]{2,1,3,0:T(8,128)(2,1)} copy(bf16[16,8,256,176]{2,0,3,1:T(8,128)(2,1)} %bitcast.5) | data formatting | bytes 23068672 | tf_op jit(solution)/shard_map/all_to_all | solution.py:20
  390.4 18.0 %all_to_all.33 = bf16[16,2048,176]{1,2,0:T(8,128)(2,1)} reshape(bf16[16,8,256,176]{2,1,3,0:T(8,128)(2,1)} %copy.24) | data formatting | bytes 23068672 | tf_op jit(solution)/shard_map/all_to_all | solution.py:20
  408.3 11.4 %copy.20 = bf16[16,8,256,176]{2,1,3,0:T(8,128)(2,1)} copy(bf16[16,8,256,176]{2,0,3,1:T(8,128)(2,1)} %bitcast.2) | data formatting | bytes 23068672 | tf_op jit(solution)/shard_map/all_to_all | solution.py:19
  419.7 18.0 %all_to_all.29 = bf16[16,2048,176]{1,2,0:T(8,128)(2,1)} reshape(bf16[16,8,256,176]{2,1,3,0:T(8,128)(2,1)} %copy.20) | data formatting | bytes 23068672 | tf_op jit(solution)/shard_map/all_to_all | solution.py:19
  437.7 0.7 copy.30
  (8 shorter events, 0.0 us)
Async XLA Ops:
  7.2 71.9 %all-reduce.3.cloned.1.call-start = ((), (), s32[]{:S(2)}) async-start(), calls=%async_computation.2 | async-start | bytes 360448 | tf_op jit(solution)/shard_map/psum | solution.py:8
  94.4 133.0 %all-to-all-start.1 = ((bf16[16,256,1408]{1,0,2:T(8,128)(2,1)}), bf16[16,256,1408]{1,0,2:T(8,128)(2,1)}, u32[]{:S(2)}, u32[]{:S(2)}) async-start(bf16[16,256,1408]{1,0,2:T(8,128)(2,1)} %divide_convert_fusion), calls=%async_computation.1 | async-start | bytes 23068672 | tf_op jit(solution)/shard_map/all_to_all | solution.py:20
  99.7 23.7 %copy-start = (f32[16,1408]{1,0:T(8,128)S(1)}, f32[16,1408]{1,0:T(8,128)}, u32[]{:S(2)}) copy-start(f32[16,1408]{1,0:T(8,128)} %get-tuple-element.5) | copy-start | bytes 270340
  123.7 109.0 %copy-start.1 = (f32[256,16]{0,1:T(8,128)S(1)}, f32[256,16]{0,1:T(8,128)}, u32[]{:S(2)}) copy-start(f32[256,16]{0,1:T(8,128)} %param.6) | copy-start | bytes 49156
  123.7 109.0 %copy-start.2 = (f32[256]{0:T(256)S(1)}, f32[256]{0:T(256)}, u32[]{:S(2)}) copy-start(f32[256]{0:T(256)} %param.7) | copy-start | bytes 3076
  227.4 180.9 %all-to-all-start = ((bf16[16,256,1408]{1,0,2:T(8,128)(2,1)}), bf16[16,256,1408]{1,0,2:T(8,128)(2,1)}, u32[]{:S(2)}, u32[]{:S(2)}) async-start(bf16[16,256,1408]{1,0,2:T(8,128)(2,1)} %divide_convert_fusion.1), calls=%async_computation | async-start | bytes 23068672 | tf_op jit(solution)/shard_map/all_to_all | solution.py:19
Sparse Core Ops, SparseCore 0:
  23.2 55.8 all-reduce.2
where the time goes:
time: 447 us; the launch traced here: 445 us
  blocking collectives  145 us (32%)
  waiting for transfers between devices  122 us (27%)
  local copies, waits for them, and re-layouts  110 us (25%)
  other arithmetic  44.3 us (10%)
  between operations  14.1 us (3%)
  starting transfers between devices  10.5 us (2%)
    all_gather x1, blocking collectives, local(): row_router = lax.all_gather(part_router, 'shard', axis=0, tiled=True)  131 us
    all_to_all x1, waiting for transfers between devices, local(): lax.all_to_all(narrow_up, 'shard', split_axis=2, concat_axis=1, tiled=True)  89.5 us
    unnamed x9, local copies, waits for them, and re-layouts  48.1 us
    psum x1, waiting for transfers between devices, local(): lax.psum((jnp.sum(master_gate * master_gate, axis=1), jnp.sum(master_up *...  32.3 us
    all_to_all x2, local copies, waits for them, and re-layouts, local(): lax.all_to_all(narrow_gate, 'shard', split_axis=2, concat_axis=1, tiled=T...  29.3 us
    all_to_all x2, local copies, waits for them, and re-layouts, local(): lax.all_to_all(narrow_up, 'shard', split_axis=2, concat_axis=1, tiled=True)  29.3 us
    reduce_sum x1, other arithmetic, local(): jnp.sum(master_up * master_up, axis=1)  15.8 us
    convert_element_type x1, other arithmetic, local(): (master_up / jnp.expand_dims(scale_up, 1)).astype(jnp.bfloat16)  14.2 us
  transfers between devices with their start and end apart: 3, of which 2 were waited for; matrix products, arithmetic and copies ran while one was open for 17% of the time, Pallas kernels for 0%

commit v1 on v0

--- a/solution.py
+++ b/solution.py
@@ -17,7 +17,12 @@
     )
     final_gate, final_up = (
         lax.all_to_all(narrow_gate, "shard", split_axis=2, concat_axis=1, tiled=True),
-        lax.all_to_all(narrow_up, "shard", split_axis=2, concat_axis=1, tiled=True),
+        jnp.concatenate(
+            lax.all_to_all(
+                jnp.stack(jnp.split(narrow_up, lax.axis_size("shard"), axis=2)), "shard", 0, 0
+            ),
+            axis=1,
+        ),
     )
     scale_gate = lax.dynamic_slice_in_dim(
         scale_gate, lax.axis_index("shard") * final_gate.shape[2], final_gate.shape[2], axis=1

time: 447 us -> 428 us (0.957)
  local copies, waits for them, and re-layouts: 110 us -> 99.3 us
  waiting for transfers between devices: 122 us -> 117 us
    all_to_all x1, waiting for transfers between devices: 89.5 us -> 0.01 us  [local(): lax.all_to_all(jnp.stack(jnp.split(narrow_up, lax.axis_size('shard'), axi...]
    all_to_all x1, waiting for transfers between devices: 0.01 us -> 84.8 us  [local(): lax.all_to_all(narrow_gate, 'shard', split_axis=2, concat_axis=1, tiled=T...]
    all_to_all x2 -> x0, local copies, waits for them, and re-layouts: 29.3 us -> none  [local(): lax.all_to_all(narrow_up, 'shard', split_axis=2, concat_axis=1, tiled=True)]
    reshape x0 -> x1, local copies, waits for them, and re-layouts: none -> 10 us  [local(): jnp.concatenate(lax.all_to_all(jnp.stack(jnp.split(narrow_up, lax.axis_si...]
    unnamed x9 -> x16, local copies, waits for them, and re-layouts: 48.1 us -> 56.2 us
  transfers between devices with their start and end apart: 3 -> 3, of which waited for: 2 -> 2; matrix products, arithmetic and copies ran while one was open for 17% -> 19% of each run, Pallas kernels for 0% -> 0%
where the time goes in v1:
time: 428 us; the launch traced here: 426 us
  blocking collectives  145 us (34%)
  waiting for transfers between devices  117 us (27%)
  local copies, waits for them, and re-layouts  99.3 us (23%)
  other arithmetic  39.9 us (9%)
  between operations  14.1 us (3%)
  starting transfers between devices  10.5 us (2%)
    all_gather x1, blocking collectives, local(): row_router = lax.all_gather(part_router, 'shard', axis=0, tiled=True)  131 us
    all_to_all x1, waiting for transfers between devices, local(): lax.all_to_all(narrow_gate, 'shard', split_axis=2, concat_axis=1, tiled=T...  84.8 us
    unnamed x16, local copies, waits for them, and re-layouts  56.2 us
    psum x1, waiting for transfers between devices, local(): lax.psum((jnp.sum(master_gate * master_gate, axis=1), jnp.sum(master_up *...  32.3 us
    all_to_all x2, local copies, waits for them, and re-layouts, local(): lax.all_to_all(narrow_gate, 'shard', split_axis=2, concat_axis=1, tiled=T...  29.3 us
    reduce_sum x1, other arithmetic, local(): jnp.sum(master_up * master_up, axis=1)  15.8 us
    convert_element_type x1, other arithmetic, local(): (master_gate / jnp.expand_dims(scale_gate, 1)).astype(jnp.bfloat16)  14.2 us
    all_gather x1, blocking collectives, local(): serve_router = lax.all_gather(row_router, 'expert', axis=1, tiled=True)  14 us
  transfers between devices with their start and end apart: 3, of which 2 were waited for; matrix products, arithmetic and copies ran while one was open for 19% of the time, Pallas kernels for 0%

profile of v1, /device:TPU:0, one launch (start us, length us, event | category | flops | bytes accessed | tf_op | source)
XLA Modules:
  0.0 425.9 jit_solution(538050658232664243)
XLA Ops:
  7.2 15.8 %multiply_reduce_fusion = (f32[16,1408]{1,0:T(8,128)}, f32[16,1408]{1,0:T(8,128)}) fusion(f32[16,256,1408]{2,1,0:T(8,128)} %param.5, f32[16,256,1408]{2,1,0:T(8,128)} %param.4), kind=kLoop, calls=%fused_computation.1 | loop fusion | flops 23023616 | bytes 46317568 | tf_op jit(solution)/shard_map/reduce_sum | solution.py:9
  23.1 23.7 %copy.22 = f32[16,256,1408]{1,0,2:T(8,128)} copy(f32[16,256,1408]{2,1,0:T(8,128)} %param.4) | data formatting | bytes 46137344 | tf_op args[0]
  46.8 32.3 %all-reduce.3.cloned.1.call-done = (f32[16,1408]{1,0:T(8,128)}, f32[16,1408]{1,0:T(8,128)}) async-done(((f32[16,1408]{1,0:T(8,128)}, f32[16,1408]{1,0:T(8,128)}), (f32[16,1408]{1,0:T(8,128)}, f32[16,1408]{1,0:T(8,128)})) %all-reduce.3.cloned.1.call-update) | async-done | bytes 180240 | tf_op jit(solution)/shard_map/psum | solution.py:8
  79.0 0.9 sqrt.6
  80.2 14.2 %divide_convert_fusion.1 = bf16[16,256,1408]{1,0,2:T(8,128)(2,1)} fusion(f32[16,256,1408]{1,0,2:T(8,128)} %copy.22, f32[16,1408]{0,1:T(8,128)S(1)} %copy.21), kind=kLoop, calls=%fused_computation.2 | loop fusion | flops 11534336 | bytes 34693120 | tf_op jit(solution)/shard_map/convert_element_type | solution.py:15
  94.4 5.2 %all-to-all-start = ((bf16[16,256,1408]{1,0,2:T(8,128)(2,1)}), bf16[16,256,1408]{1,0,2:T(8,128)(2,1)}, u32[]{:S(2)}, u32[]{:S(2)}) async-start(bf16[16,256,1408]{1,0,2:T(8,128)(2,1)} %divide_convert_fusion.1), calls=%async_computation | async-start | bytes 23068672 | tf_op jit(solution)/shard_map/all_to_all | solution.py:19
  99.7 23.4 %copy.25 = f32[16,256,1408]{1,2,0:T(8,128)} copy(f32[16,256,1408]{2,1,0:T(8,128)} %param.5) | data formatting | bytes 46137344 | tf_op args[1]
  123.1 9.8 %divide_convert_fusion = bf16[16,256,1408]{1,2,0:T(8,128)(2,1)S(1)} fusion(f32[16,256,1408]{1,2,0:T(8,128)} %copy.25, f32[16,1408]{1,0:T(8,128)S(1)} %sqrt.7), kind=kLoop, calls=%fused_computation | loop fusion | flops 11534336 | bytes 34693120 | tf_op jit(solution)/shard_map/convert_element_type | solution.py:16
  132.9 1.2 fusion.7
  134.1 1.2 fusion.6
  135.4 1.2 fusion.5
  136.6 1.2 fusion.4
  137.8 1.2 fusion.3
  139.0 1.2 fusion.2
  140.2 1.2 fusion.1
  141.4 1.2 fusion
  142.6 84.8 %all-to-all-done = bf16[16,256,1408]{1,0,2:T(8,128)(2,1)} async-done(((bf16[16,256,1408]{1,0,2:T(8,128)(2,1)}), bf16[16,256,1408]{1,0,2:T(8,128)(2,1)}, u32[]{:S(2)}, u32[]{:S(2)}) %all-to-all-start) | async-done | bytes 11534368 | tf_op jit(solution)/shard_map/all_to_all | solution.py:19
  227.4 5.3 %all-to-all-start.1 = ((bf16[8,16,256,176]{2,3,1,0:T(8,128)(2,1)}), bf16[8,16,256,176]{2,3,1,0:T(8,128)(2,1)}, u32[]{:S(2)}, u32[]{:S(2)}) async-start(bf16[8,16,256,176]{2,3,1,0:T(8,128)(2,1)} %fusion), calls=%async_computation.1 | async-start | bytes 23068672 | tf_op jit(solution)/shard_map/all_to_all | solution.py:21
  232.7 130.9 %all_gather.6 = bf16[2048,16]{0,1:T(8,128)(2,1)S(1)} all-gather(bf16[256,16]{0,1:T(8,128)(2,1)S(1)} %multiply_convert_fusion), channel_id=1, replica_groups=mesh['expert'=4,'shard'=8] {'shard'}, dimensions={0}, use_global_device_ids=true | all-gather | bytes 73728 | tf_op jit(solution)/shard_map/all_gather | solution.py:34
  363.6 14.0 %all_gather.7 = bf16[2048,64]{0,1:T(8,128)(2,1)S(1)} all-gather(bf16[2048,16]{0,1:T(8,128)(2,1)S(1)} %all_gather.6), channel_id=1, replica_groups=mesh['expert'=4,'shard'=8] {'expert'}, dimensions={1}, use_global_device_ids=true | all-gather | bytes 327680 | tf_op jit(solution)/shard_map/all_gather | solution.py:35
  379.0 11.3 %copy.24 = bf16[16,8,256,176]{2,1,3,0:T(8,128)(2,1)} copy(bf16[16,8,256,176]{2,0,3,1:T(8,128)(2,1)} %bitcast.2) | data formatting | bytes 23068672 | tf_op jit(solution)/shard_map/all_to_all | solution.py:19
  390.3 18.0 %all_to_all.19 = bf16[16,2048,176]{1,2,0:T(8,128)(2,1)} reshape(bf16[16,8,256,176]{2,1,3,0:T(8,128)(2,1)} %copy.24) | data formatting | bytes 23068672 | tf_op jit(solution)/shard_map/all_to_all | solution.py:19
  408.3 10.0 %copy.28 = bf16[8,16,22,8,256]{4,3,0,2,1:T(8,128)(2,1)} copy(bf16[8,16,22,8,256]{4,3,2,1,0:T(8,128)(2,1)} %bitcast.12) | data formatting | bytes 23068672 | tf_op jit(solution)/shard_map/reshape | solution.py:20
  418.3 0.7 copy.39
  (14 shorter events, 1.7 us)
Async XLA Ops:
  7.2 71.9 %all-reduce.3.cloned.1.call-start = ((), (), s32[]{:S(2)}) async-start(), calls=%async_computation.2 | async-start | bytes 360448 | tf_op jit(solution)/shard_map/psum | solution.py:8
  94.4 133.0 %all-to-all-start = ((bf16[16,256,1408]{1,0,2:T(8,128)(2,1)}), bf16[16,256,1408]{1,0,2:T(8,128)(2,1)}, u32[]{:S(2)}, u32[]{:S(2)}) async-start(bf16[16,256,1408]{1,0,2:T(8,128)(2,1)} %divide_convert_fusion.1), calls=%async_computation | async-start | bytes 23068672 | tf_op jit(solution)/shard_map/all_to_all | solution.py:19
  99.7 23.4 %copy-start = (f32[16,1408]{1,0:T(8,128)S(1)}, f32[16,1408]{1,0:T(8,128)}, u32[]{:S(2)}) copy-start(f32[16,1408]{1,0:T(8,128)} %get-tuple-element.6) | copy-start | bytes 270340
  142.6 90.1 %copy-start.1 = (f32[256,16]{0,1:T(8,128)S(1)}, f32[256,16]{0,1:T(8,128)}, u32[]{:S(2)}) copy-start(f32[256,16]{0,1:T(8,128)} %param.6) | copy-start | bytes 49156
  142.6 90.1 %copy-start.2 = (f32[256]{0:T(256)S(1)}, f32[256]{0:T(256)}, u32[]{:S(2)}) copy-start(f32[256]{0:T(256)} %param.7) | copy-start | bytes 3076
  227.4 180.9 %all-to-all-start.1 = ((bf16[8,16,256,176]{2,3,1,0:T(8,128)(2,1)}), bf16[8,16,256,176]{2,3,1,0:T(8,128)(2,1)}, u32[]{:S(2)}, u32[]{:S(2)}) async-start(bf16[8,16,256,176]{2,3,1,0:T(8,128)(2,1)} %fusion), calls=%async_computation.1 | async-start | bytes 23068672 | tf_op jit(solution)/shard_map/all_to_all | solution.py:21
Sparse Core Ops, SparseCore 0:
  23.2 55.8 all-reduce.2
